TPU v7x, 32 devices: a whole 2x2x4 slice. The times are simulated.
32 devices in a mesh: seq: 8 (over z, core), mp: 4 (over y, x).
Axes of the slice: x: 2, y: 2, z: 4, core: 2. Of those that a mesh axis runs over, the one named last changes fastest.
Arguments:
- hidden_in: bfloat16 [4096, 4096], P('seq', 'mp'), may hold values from -30 to 30
- norm_gain: float32 [4096], replicated, may hold values from 0.1 to 1.9
- w_z: bfloat16 [4096, 8192], P('seq', 'mp'), may hold values from -0.09375 to 0.09375
- w_x: bfloat16 [4096, 8192], P('seq', 'mp'), may hold values from -0.09375 to 0.09375
- w_b: bfloat16 [4096, 1024], P('seq', 'mp'), may hold values from -0.09375 to 0.09375
- w_c: bfloat16 [4096, 1024], P('seq', 'mp'), may hold values from -0.09375 to 0.09375
- w_dt: bfloat16 [4096, 128], P('seq', 'mp'), may hold values from -0.0625 to 0.0625
- conv_x: float32 [4, 8192], P(None, 'mp'), may hold values from -3 to 3
- conv_b: float32 [4, 1024], P(None, 'mp'), may hold values from -3 to 3
- conv_c: float32 [4, 1024], P(None, 'mp'), may hold values from -3 to 3
- dt_bias: float32 [128], P('mp'), may hold values from -9 to -5
- a_rate: float32 [128], P('mp'), may hold values from 0.5 to 16
- skip_gain: float32 [128], P('mp'), may hold values from -3 to 3
- group_gain: float32 [8192], P('mp'), may hold values from 0.1 to 1.9
- w_out: bfloat16 [8192, 4096], P('mp', 'seq'), may hold values from -0.0625 to 0.0625
- attn_gain: float32 [4096], replicated, may hold values from 0.1 to 1.9
- w_q: bfloat16 [4096, 4096], P(None, 'mp'), may hold values from -0.125 to 0.125
- w_k: bfloat16 [4096, 1024], P(None, 'mp'), may hold values from -0.125 to 0.125
- w_v: bfloat16 [4096, 1024], P(None, 'mp'), may hold values from -0.09375 to 0.09375
Outputs:
- mixed: float32 [4096, 4096], P('seq', 'mp')
- context: float32 [4096, 4096], P('seq', 'mp')
All inputs are finite; a program needn't handle non-finite values.
Results may differ from a plain program's by a relative error of at most 0.017.
Values may be sent and summed in bfloat16 or wider, within the bound.
A program may use at most 192 MiB of HBM per device.

v0:
```python
import jax
import jax.numpy as jnp
from jax import lax
from jax.sharding import PartitionSpec as P

P_SIZE = 64
N = 128
HD = 128
WINDOW = 4096
QB = 128


HIGH = lax.Precision.HIGHEST


def from_behind(block, axis, distance):
    devices = range(lax.axis_size(axis))
    route = [(i - distance, i) for i in devices if i - distance in devices]
    return lax.ppermute(block, axis, route)


def rms_norm(values, gain):
    return values * lax.rsqrt(jnp.mean(values * values, axis=-1, keepdims=True) + 1e-05) * gain


def causal_conv(values, rim, device_routine):
    padded = jnp.concatenate([rim, values], axis=0)
    length = values.shape[0]
    summed = jnp.zeros(values.shape, jnp.float32)
    for offset in range(device_routine.shape[0]):
        summed = summed + device_routine[offset][None, :] * padded[offset : offset + length]
    return jax.nn.silu(summed)


def ssd_block(carry_state, pieces):
    inputs, step_sizes, decays, keys_b, reads_c = pieces
    per_group = inputs.shape[1] // keys_b.shape[1]
    b_heads = jnp.repeat(keys_b, per_group, axis=1)
    c_heads = jnp.repeat(reads_c, per_group, axis=1)
    cumulative = jnp.cumsum(decays, axis=0)
    length = inputs.shape[0]
    causal_mask = jnp.arange(length)[:, None] >= jnp.arange(length)[None, :]
    spread = cumulative[:, None, :] - cumulative[None, :, :]
    within = jnp.exp(jnp.where(causal_mask[:, :, None], spread, -jnp.inf))
    affinity = jnp.einsum("tgn,sgn->gts", reads_c, keys_b, precision=HIGH)
    affinity = jnp.repeat(affinity, per_group, axis=0)
    mixing = affinity * jnp.transpose(within, (2, 0, 1)) * jnp.transpose(step_sizes)[:, None, :]
    inside = jnp.einsum("hts,shp->thp", mixing, inputs, precision=HIGH)
    carried = jnp.exp(cumulative)[:, :, None] * jnp.einsum(
        "thn,hpn->thp", c_heads, carry_state, precision=HIGH
    )
    tail_weight = jnp.exp(cumulative[-1][None, :] - cumulative) * step_sizes
    fresh_state = jnp.einsum("sh,shp,shn->hpn", tail_weight, inputs, b_heads, precision=HIGH)
    updated = jnp.exp(cumulative[-1])[:, None, None] * carry_state + fresh_state
    return (updated, inside + carried)


def run_ssd(inputs, step_sizes, decays, keys_b, reads_c, block, carry_state):
    total_rows = inputs.shape[0]
    block_count = total_rows // block

    def blocked(values):
        return values.reshape((block_count, block) + values.shape[1:])

    final_state, outputs = lax.scan(
        ssd_block,
        carry_state,
        (blocked(inputs), blocked(step_sizes), blocked(decays), blocked(keys_b), blocked(reads_c)),
    )
    return (final_state, outputs.reshape((total_rows,) + outputs.shape[2:]))


def window_attention(asking_vectors, keys, values, shift_rows, first_key):
    per_kv = asking_vectors.shape[1] // keys.shape[1]
    keys_all = jnp.repeat(keys, per_kv, axis=1)
    values_all = jnp.repeat(values, per_kv, axis=1)
    query_rows = asking_vectors.shape[0]
    key_count = keys.shape[0]
    scale = asking_vectors.shape[2] ** (-0.5)
    index_offsets = jnp.arange(key_count)[None, :] - shift_rows - jnp.arange(query_rows)[:, None]
    allowed = (
        (index_offsets <= 0)
        & (index_offsets > -WINDOW)
        & (first_key + jnp.arange(key_count) >= 0)[None, :]
    )

    def one_head(operands):
        query_h, key_h, value_h = operands
        scores = (
            lax.dot_general(
                query_h, key_h, (((1,), (1,)), ((), ())), preferred_element_type=jnp.float32
            )
            * scale
        )
        scores = jnp.where(allowed, scores, -jnp.inf)
        row_peak = jnp.max(scores, axis=1, keepdims=True)
        exp_scores = jnp.exp(scores - row_peak)
        weights = (exp_scores / jnp.sum(exp_scores, axis=1, keepdims=True)).astype(jnp.bfloat16)
        return jnp.dot(weights, value_h, preferred_element_type=jnp.float32)

    outputs = lax.map(
        one_head,
        (
            jnp.transpose(asking_vectors, (1, 0, 2)),
            jnp.transpose(keys_all, (1, 0, 2)),
            jnp.transpose(values_all, (1, 0, 2)),
        ),
    )
    return jnp.transpose(outputs, (1, 0, 2)).reshape(query_rows, -1)


def on_device(
    hidden_in,
    norm_gain,
    w_z,
    w_x,
    w_b,
    w_c,
    w_dt,
    conv_x,
    conv_b,
    conv_c,
    dt_bias,
    a_rate,
    skip_gain,
    group_gain,
    w_out,
    attn_gain,
    w_q,
    w_k,
    w_v,
):
    rows_here = hidden_in.shape[0]
    whole_rows = lax.all_gather(hidden_in, "mp", axis=1, tiled=True)
    normed = rms_norm(whole_rows.astype(jnp.float32), norm_gain).astype(jnp.bfloat16)

    def add_rows(piece):
        return jnp.dot(normed, piece, preferred_element_type=jnp.float32)

    pieces = (
        lax.all_gather(w_z, "seq", axis=0, tiled=True),
        lax.all_gather(w_x, "seq", axis=0, tiled=True),
        lax.all_gather(w_b, "seq", axis=0, tiled=True),
        lax.all_gather(w_c, "seq", axis=0, tiled=True),
        lax.all_gather(w_dt, "seq", axis=0, tiled=True),
    )
    gate_proj, input_mapped, b_proj, c_proj, delta_time_unscaled = tuple(
        (add_rows(piece) for piece in pieces)
    )
    rim_rows = conv_x.shape[0] - 1
    rims = from_behind(
        (
            input_mapped[rows_here - rim_rows :],
            b_proj[rows_here - rim_rows :],
            c_proj[rows_here - rim_rows :],
        ),
        "seq",
        1,
    )
    conv_in = causal_conv(input_mapped, rims[0], conv_x)
    conv_bv = causal_conv(b_proj, rims[1], conv_b)
    conv_cv = causal_conv(c_proj, rims[2], conv_c)
    step_sizes = jax.nn.softplus(delta_time_unscaled + dt_bias[None, :])
    decays = -a_rate[None, :] * step_sizes
    heads_here = dt_bias.shape[0]
    groups_here = conv_b.shape[1] // N
    inputs = conv_in.reshape(rows_here, heads_here, P_SIZE)
    keys_b = conv_bv.reshape(rows_here, groups_here, N)
    reads_c = conv_cv.reshape(rows_here, groups_here, N)
    start_state = jnp.zeros((heads_here, P_SIZE, N), jnp.float32)
    local_state, ssd_out = run_ssd(inputs, step_sizes, decays, keys_b, reads_c, QB, start_state)
    cumulative = jnp.cumsum(decays, axis=0)
    decay_total = jnp.exp(cumulative[-1])

    def relay_state(turn, incoming):
        return from_behind(decay_total[:, None, None] * incoming + local_state, "seq", 1)

    incoming = lax.fori_loop(0, lax.axis_size("seq") - 1, relay_state, start_state)
    c_heads = jnp.repeat(reads_c, heads_here // groups_here, axis=1)
    ssd_out = ssd_out + jnp.exp(cumulative)[:, :, None] * jnp.einsum(
        "thn,hpn->thp", c_heads, incoming, precision=HIGH
    )
    full = ssd_out + skip_gain[None, :, None] * inputs
    gated = full.reshape(rows_here, -1) * jax.nn.silu(gate_proj)
    grouped = gated.reshape(rows_here, groups_here, -1)
    y_normed = (
        rms_norm(grouped, group_gain.reshape(groups_here, -1))
        .reshape(rows_here, -1)
        .astype(jnp.bfloat16)
    )
    terms = jnp.dot(
        y_normed,
        lax.all_gather(w_out, "seq", axis=1, tiled=True),
        preferred_element_type=jnp.float32,
    )
    rounded = lax.optimization_barrier(terms.astype(jnp.bfloat16)).astype(jnp.float32)
    summed = lax.psum_scatter(
        rounded.astype(jnp.bfloat16), "mp", scatter_dimension=1, tiled=True
    ).astype(jnp.float32)
    mixed = hidden_in.astype(jnp.float32) + summed
    mixed_low = mixed.astype(jnp.bfloat16)
    stream_rows = lax.all_gather(mixed_low, "mp", axis=1, tiled=True)
    normed_two = rms_norm(stream_rows.astype(jnp.float32), attn_gain).astype(jnp.bfloat16)
    asking_vectors = jnp.dot(normed_two, w_q, preferred_element_type=jnp.float32).astype(
        jnp.bfloat16
    )
    own_keys = jnp.dot(normed_two, w_k, preferred_element_type=jnp.float32).astype(jnp.bfloat16)
    own_values = jnp.dot(normed_two, w_v, preferred_element_type=jnp.float32).astype(jnp.bfloat16)
    reach = WINDOW // rows_here
    key_parts = [own_keys]
    value_parts = [own_values]
    moving = (own_keys, own_values)
    for distance in range(reach):
        moving = from_behind((moving[0], moving[1]), "seq", 1)
        key_parts.insert(0, moving[0])
        value_parts.insert(0, moving[1])
    kv_heads = own_keys.shape[1] // HD
    key_rows = jnp.concatenate(key_parts, axis=0).reshape(-1, kv_heads, HD)
    value_rows = jnp.concatenate(value_parts, axis=0).reshape(-1, kv_heads, HD)
    first_key = lax.axis_index("seq") * rows_here - reach * rows_here
    context = window_attention(
        asking_vectors.reshape(rows_here, -1, HD),
        key_rows,
        value_rows,
        reach * rows_here,
        first_key,
    )
    return (mixed, context)


def solution(mesh):
    placed = (
        P("seq", "mp"),
        P(),
        P("seq", "mp"),
        P("seq", "mp"),
        P("seq", "mp"),
        P("seq", "mp"),
        P("seq", "mp"),
        P(None, "mp"),
        P(None, "mp"),
        P(None, "mp"),
        P("mp"),
        P("mp"),
        P("mp"),
        P("mp"),
        P("mp", "seq"),
        P(),
        P(None, "mp"),
        P(None, "mp"),
        P(None, "mp"),
    )
    return jax.shard_map(
        on_device,
        mesh=mesh,
        in_specs=placed,
        out_specs=(P("seq", "mp"), P("seq", "mp")),
        check_vma=False,
    )
```

profile of v0, /device:TPU:25, one launch (start us, length us, event | category | flops | bytes accessed | tf_op | source)
XLA Modules:
  0.0 1053.8 jit_solution(144344932053063011)
XLA Ops:
  11.8 14.7 %all_gather.25 = bf16[4096,32]{0,1:T(8,128)(2,1)S(1)} all-gather(bf16[512,32]{0,1:T(8,128)(2,1)S(1)} %copy-done.28), channel_id=1, replica_groups=mesh['seq'=8,'mp'=4] {'seq'}, dimensions={0}, use_global_device_ids=true | all-gather | bytes 294912 | tf_op jit(solution)/shard_map/all_gather | solution.py:145
  28.4 34.9 %all-gather.8.cloned.1.call-done = bf16[512,4096]{1,0:T(8,128)(2,1)} async-done(((bf16[512,1024]{1,0:T(8,128)(2,1)}), bf16[512,4096]{1,0:T(8,128)(2,1)}) %all-gather.8.cloned.1.call-update) | async-done | bytes 4194320 | tf_op jit(solution)/shard_map/all_gather | solution.py:134
  66.4 26.7 %all-gather.14.cloned.1.call-done = bf16[4096,256]{1,0:T(8,128)(2,1)} async-done(((bf16[512,256]{1,0:T(8,128)(2,1)}), bf16[4096,256]{1,0:T(8,128)(2,1)}) %all-gather.14.cloned.1.call-update) | async-done | bytes 2097168 | tf_op jit(solution)/shard_map/all_gather | solution.py:144
  100.0 23.3 %all-gather.12.cloned.1.call-done = bf16[4096,256]{1,0:T(8,128)(2,1)} async-done(((bf16[512,256]{1,0:T(8,128)(2,1)}), bf16[4096,256]{1,0:T(8,128)(2,1)}) %all-gather.12.cloned.1.call-update) | async-done | bytes 2097168 | tf_op jit(solution)/shard_map/all_gather | solution.py:143
  141.9 131.9 %all-gather.10.cloned.1.call-done = bf16[4096,2048]{1,0:T(8,128)(2,1)} async-done(((bf16[512,2048]{1,0:T(8,128)(2,1)}), bf16[4096,2048]{1,0:T(8,128)(2,1)}) %all-gather.10.cloned.1.call-update) | async-done | bytes 16777232 | tf_op jit(solution)/shard_map/all_gather | solution.py:142
  273.8 13.4 %fusion.89 = f32[512,2048]{1,0:T(8,128)S(1)} fusion(bf16[4096,2048]{1,0:T(8,128)(2,1)} %all-gather.10.cloned.1.call-done, bf16[512,4096]{1,0:T(8,128)(2,1)} %all-gather.8.cloned.1.call-done, f32[4096]{0:T(1024)} %param.26, f32[512]{0:T(512)} %copy-done.35), kind=kOutput, calls=%fused_computation.160 | convolution fusion | flops 8598323200 | bytes 25184256 | tf_op jit(solution)/shard_map/dot_general | solution.py:138
  326.7 210.4 %while.36 = (s32[]{:T(128)}, f32[32,64,128]{2,1,0:T(8,128)S(1)}, f32[4,128,32,64]{1,0,3,2:T(4,128)}, f32[4,128,32]{2,1,0:T(8,128)}, f32[4,128,32]{2,1,0:T(8,128)...) while((s32[]{:T(128)}, f32[32,64,128]{2,1,0:T(8,128)S(1)}, ...), condition=%wide.region_3.4_spmd.clone, body=%wide.region_1.3_spmd.clone.sunk | while | flops 1262768128 | bytes 25823172 | solution.py:65
  348.8 26.5 %dynamic_update_slice.14 = f32[4,128,32,64]{1,0,3,2:T(4,128)} dynamic-update-slice(f32[4,128,32,64]{1,0,3,2:T(4,128)} %get-tuple-element.399, f32[1,128,32,64]{1,0,3,2:T(1,128)} %bitcast.225, s32[]{:T(128)} %get-tuple-element.397, s32[]{:T(128)} %constant.78.clone.1..sunk, s32[]{:T(128)} %constant.78.clone.1..sunk, s32[]{:T(128)} %constant.78.clone.1..sunk) | dynamic-update-slice | bytes 2097156 | tf_op jit(solution)/shard_map/while/body/jit(dynamic_update_index_in_dim)/dynamic_update_slice | solution.py:65
  401.4 26.5 %dynamic_update_slice.14 = f32[4,128,32,64]{1,0,3,2:T(4,128)} dynamic-update-slice(f32[4,128,32,64]{1,0,3,2:T(4,128)} %get-tuple-element.399, f32[1,128,32,64]{1,0,3,2:T(1,128)} %bitcast.225, s32[]{:T(128)} %get-tuple-element.397, s32[]{:T(128)} %constant.78.clone.1..sunk, s32[]{:T(128)} %constant.78.clone.1..sunk, s32[]{:T(128)} %constant.78.clone.1..sunk) | dynamic-update-slice | bytes 2097156 | tf_op jit(solution)/shard_map/while/body/jit(dynamic_update_index_in_dim)/dynamic_update_slice | solution.py:65
  454.2 26.5 %dynamic_update_slice.14 = f32[4,128,32,64]{1,0,3,2:T(4,128)} dynamic-update-slice(f32[4,128,32,64]{1,0,3,2:T(4,128)} %get-tuple-element.399, f32[1,128,32,64]{1,0,3,2:T(1,128)} %bitcast.225, s32[]{:T(128)} %get-tuple-element.397, s32[]{:T(128)} %constant.78.clone.1..sunk, s32[]{:T(128)} %constant.78.clone.1..sunk, s32[]{:T(128)} %constant.78.clone.1..sunk) | dynamic-update-slice | bytes 2097156 | tf_op jit(solution)/shard_map/while/body/jit(dynamic_update_index_in_dim)/dynamic_update_slice | solution.py:65
  506.8 26.5 %dynamic_update_slice.14 = f32[4,128,32,64]{1,0,3,2:T(4,128)} dynamic-update-slice(f32[4,128,32,64]{1,0,3,2:T(4,128)} %get-tuple-element.399, f32[1,128,32,64]{1,0,3,2:T(1,128)} %bitcast.225, s32[]{:T(128)} %get-tuple-element.397, s32[]{:T(128)} %constant.78.clone.1..sunk, s32[]{:T(128)} %constant.78.clone.1..sunk, s32[]{:T(128)} %constant.78.clone.1..sunk) | dynamic-update-slice | bytes 2097156 | tf_op jit(solution)/shard_map/while/body/jit(dynamic_update_index_in_dim)/dynamic_update_slice | solution.py:65
  543.6 142.1 %while.34 = (s32[]{:T(128)}, f32[32,64,128]{2,1,0:T(8,128)}, f32[32]{0:T(128)S(1)}, f32[32,64,128]{2,1,0:T(8,128)S(1)}, s32[]{:T(128)}) while((s32[]{:T(128)}, f32[32,64,128]{2,1,0:T(8,128)}, f32[32]{0:T(128)S(1)}, f32[32,64,128]{2,1,0:T(8,128)S(1)}, s32[]{:T(128)}) %tuple.115), condition=%wide.region_7.8_spmd, body=%wide.region_6.7_spmd.sunk | while | flops 524290 | bytes 7340261 | solution.py:178
  558.7 33.2 %collective-permute-done = f32[32,64,128]{2,1,0:T(8,128)} collective-permute-done((f32[32,64,128]{2,1,0:T(8,128)}, f32[32,64,128]{2,1,0:T(8,128)}, u32[]{:S(2)}, u32[]{:S(2)}) %collective-permute-start) | collective-permute-done | bytes 1048608 | tf_op jit(solution)/shard_map/while/body/eval_jaxpr/ppermute | solution.py:19
  595.5 15.1 %collective-permute-done = f32[32,64,128]{2,1,0:T(8,128)} collective-permute-done((f32[32,64,128]{2,1,0:T(8,128)}, f32[32,64,128]{2,1,0:T(8,128)}, u32[]{:S(2)}, u32[]{:S(2)}) %collective-permute-start) | collective-permute-done | bytes 1048608 | tf_op jit(solution)/shard_map/while/body/eval_jaxpr/ppermute | solution.py:19
  614.3 15.1 %collective-permute-done = f32[32,64,128]{2,1,0:T(8,128)} collective-permute-done((f32[32,64,128]{2,1,0:T(8,128)}, f32[32,64,128]{2,1,0:T(8,128)}, u32[]{:S(2)}, u32[]{:S(2)}) %collective-permute-start) | collective-permute-done | bytes 1048608 | tf_op jit(solution)/shard_map/while/body/eval_jaxpr/ppermute | solution.py:19
  633.0 15.1 %collective-permute-done = f32[32,64,128]{2,1,0:T(8,128)} collective-permute-done((f32[32,64,128]{2,1,0:T(8,128)}, f32[32,64,128]{2,1,0:T(8,128)}, u32[]{:S(2)}, u32[]{:S(2)}) %collective-permute-start) | collective-permute-done | bytes 1048608 | tf_op jit(solution)/shard_map/while/body/eval_jaxpr/ppermute | solution.py:19
  651.8 15.1 %collective-permute-done = f32[32,64,128]{2,1,0:T(8,128)} collective-permute-done((f32[32,64,128]{2,1,0:T(8,128)}, f32[32,64,128]{2,1,0:T(8,128)}, u32[]{:S(2)}, u32[]{:S(2)}) %collective-permute-start) | collective-permute-done | bytes 1048608 | tf_op jit(solution)/shard_map/while/body/eval_jaxpr/ppermute | solution.py:19
  670.6 15.1 %collective-permute-done = f32[32,64,128]{2,1,0:T(8,128)} collective-permute-done((f32[32,64,128]{2,1,0:T(8,128)}, f32[32,64,128]{2,1,0:T(8,128)}, u32[]{:S(2)}, u32[]{:S(2)}) %collective-permute-start) | collective-permute-done | bytes 1048608 | tf_op jit(solution)/shard_map/while/body/eval_jaxpr/ppermute | solution.py:19
  689.4 12.1 %fusion.52 = f32[512,32,64]{0,2,1:T(8,128)} fusion(f32[512,32,64]{0,2,1:T(8,128)S(1)} %copy-done.3, f32[512,32,64]{0,2,1:T(8,128)S(1)} %bitcast.227, f32[32]{0:T(128)S(1)} %copy-done.37, f32[512,32]{0,1:T(8,128)S(1)} %copy-done.13, f32[512,32,128]{2,0,1:T(8,128)S(1)} %bitcast.226, f32[32,64,128]{2,1,0:T(8,128)} %get-tuple-element.101), kind=kOutput, calls=%fused_computation.75 | convolution fusion | flops 1614807040 | bytes 22085760 | tf_op jit(solution)/shard_map/thn,hpn->thp/dot_general | solution.py:180
  706.9 17.1 %fusion.79 = (f32[512,2048]{1,0:T(8,128)}, f32[512,2048]{1,0:T(8,128)}) fusion(f32[512,2048]{1,0:T(8,128)} %copy.121, bf16[4096,2048]{1,0:T(8,128)(2,1)} %all-gather.16.cloned.1.call-done, bf16[512,4096]{1,0:T(8,128)(2,1)} %all-gather.8.cloned.1.call-done, f32[4096]{0:T(1024)S(1)} %copy-done.41, f32[512]{0:T(512)S(1)} %copy-done.36), kind=kOutput, calls=%fused_computation.156 | convolution fusion | flops 8604614656 | bytes 33572864 | tf_op jit(solution)/shard_map/dot_general | solution.py:138
  739.2 18.3 %convolution_convert_fusion = bf16[512,4096]{1,0:T(8,128)(2,1)} fusion(bf16[2048,4096]{1,0:T(8,128)(2,1)} %all-gather.18.cloned.1.call-done, f32[512,2048]{1,0:T(8,128)} %bitcast.235, f32[2048]{0:T(1024)S(1)} %copy-done.43, f32[512,2048]{1,0:T(8,128)} %copy.121, f32[512,2048]{1,0:T(8,128)} %get-tuple-element.252), kind=kOutput, calls=%fused_computation.63 | convolution fusion | flops 8600420352 | bytes 33562624 | tf_op jit(solution)/shard_map/dot_general | solution.py:191
  757.6 64.8 %reduce-scatter.2.cloned.1.call-done = bf16[512,1024]{1,0:T(8,128)(2,1)} async-done(((bf16[512,4096]{1,0:T(8,128)(2,1)}), bf16[512,1024]{1,0:T(8,128)(2,1)}) %reduce-scatter.2.cloned.1.call-update) | async-done | bytes 1048592 | tf_op jit(solution)/shard_map/reduce_scatter | solution.py:197
  825.8 52.7 %all-gather.20.cloned.1.call-done = bf16[512,4096]{1,0:T(8,128)(2,1)} async-done(((bf16[512,1024]{1,0:T(8,128)(2,1)}), bf16[512,4096]{1,0:T(8,128)(2,1)}) %all-gather.20.cloned.1.call-update) | async-done | bytes 4194320 | tf_op jit(solution)/shard_map/all_gather | solution.py:202
  963.4 80.0 %while.35 = (s32[]{:T(128)}, f32[8,512,128]{2,1,0:T(8,128)}, bf16[8,512,128]{2,1,0:T(8,128)(2,1)S(1)}, bf16[8,4608,128]{2,1,0:T(8,128)(2,1)}, bf16[8,4608,128]{2...) while((s32[]{:T(128)}, f32[8,512,128]{2,1,0:T(8,128)}, ...), condition=%wide.region_14.15_spmd.clone, body=%wide.region_11.14_spmd.clone.sunk | while | flops 1238629376 | bytes 31102036 | solution.py:101
  (352 shorter events, 413.1 us)
Async XLA Ops:
  7.2 56.1 %all-gather.8.cloned.1.call-start = ((), (), s32[]{:S(2)}) async-start(), calls=%async_computation.1 | async-start | bytes 5242880 | tf_op jit(solution)/shard_map/all_gather | solution.py:134
  8.0 85.2 %all-gather.14.cloned.1.call-start = ((), (), s32[]{:S(2)}) async-start(), calls=%async_computation.4 | async-start | bytes 2359296 | tf_op jit(solution)/shard_map/all_gather | solution.py:144
  8.7 114.6 %all-gather.12.cloned.1.call-start = ((), (), s32[]{:S(2)}) async-start(), calls=%async_computation.3 | async-start | bytes 2359296 | tf_op jit(solution)/shard_map/all_gather | solution.py:143
  9.5 264.3 %all-gather.10.cloned.1.call-start = ((), (), s32[]{:S(2)}) async-start(), calls=%async_computation.2 | async-start | bytes 18874368 | tf_op jit(solution)/shard_map/all_gather | solution.py:142
  10.0 696.8 %all-gather.16.cloned.1.call-start = ((), (), s32[]{:S(2)}) async-start(), calls=%async_computation.5 | async-start | bytes 18874368 | tf_op jit(solution)/shard_map/all_gather | solution.py:141
  10.6 728.6 %all-gather.18.cloned.1.call-start = ((), (), s32[]{:S(2)}) async-start(), calls=%async_computation.6 | async-start | bytes 18874368 | tf_op jit(solution)/shard_map/all_gather | solution.py:193
  11.2 811.2 %reduce-scatter.2.cloned.1.call-start = ((), (), s32[]{:S(2)}) async-start(), calls=%async_computation.7 | async-start | bytes 5242880 | tf_op jit(solution)/shard_map/reduce_scatter | solution.py:197
  98.7 37.3 %collective-permute-start.3 = (f32[3,256]{1,0:T(4,128)}, f32[3,256]{1,0:T(4,128)}, u32[]{:S(2)}, u32[]{:S(2)}) collective-permute-start(f32[3,256]{1,0:T(4,128)} %slice.124), channel_id=1, source_target_pairs={{0,4},{4,8},{8,12},{12,16},{16,20},{20,24},{24,28},{1,5},{5,9},{9,... | collective-permute-start | bytes 9224 | tf_op jit(solution)/shard_map/ppermute | solution.py:19
  128.3 10.6 %collective-permute-start.2 = (f32[3,256]{1,0:T(4,128)}, f32[3,256]{1,0:T(4,128)}, u32[]{:S(2)}, u32[]{:S(2)}) collective-permute-start(f32[3,256]{1,0:T(4,128)} %slice.119), channel_id=1, source_target_pairs={{0,4},{4,8},{8,12},{12,16},{16,20},{20,24},{24,28},{1,5},{5,9},{9,... | collective-permute-start | bytes 9224 | tf_op jit(solution)/shard_map/ppermute | solution.py:19
  546.0 9.0 collective-permute-start
  557.4 34.4 %collective-permute-start = (f32[32,64,128]{2,1,0:T(8,128)}, f32[32,64,128]{2,1,0:T(8,128)}, u32[]{:S(2)}, u32[]{:S(2)}) collective-permute-start(f32[32,64,128]{2,1,0:T(8,128)} %multiply_add_fusion.2), channel_id=1, source_target_pairs={{0,4},{4,8},{8,12},{12,16},{16,20},{20,24},{24,28},{1,5},{5,9},{9,... | collective-permute-start | bytes 3145736 | tf_op jit(solution)/shard_map/while/body/eval_jaxpr/ppermute | solution.py:19
  594.2 16.4 %collective-permute-start = (f32[32,64,128]{2,1,0:T(8,128)}, f32[32,64,128]{2,1,0:T(8,128)}, u32[]{:S(2)}, u32[]{:S(2)}) collective-permute-start(f32[32,64,128]{2,1,0:T(8,128)} %multiply_add_fusion.2), channel_id=1, source_target_pairs={{0,4},{4,8},{8,12},{12,16},{16,20},{20,24},{24,28},{1,5},{5,9},{9,... | collective-permute-start | bytes 3145736 | tf_op jit(solution)/shard_map/while/body/eval_jaxpr/ppermute | solution.py:19
  613.0 16.4 %collective-permute-start = (f32[32,64,128]{2,1,0:T(8,128)}, f32[32,64,128]{2,1,0:T(8,128)}, u32[]{:S(2)}, u32[]{:S(2)}) collective-permute-start(f32[32,64,128]{2,1,0:T(8,128)} %multiply_add_fusion.2), channel_id=1, source_target_pairs={{0,4},{4,8},{8,12},{12,16},{16,20},{20,24},{24,28},{1,5},{5,9},{9,... | collective-permute-start | bytes 3145736 | tf_op jit(solution)/shard_map/while/body/eval_jaxpr/ppermute | solution.py:19
  631.8 16.4 %collective-permute-start = (f32[32,64,128]{2,1,0:T(8,128)}, f32[32,64,128]{2,1,0:T(8,128)}, u32[]{:S(2)}, u32[]{:S(2)}) collective-permute-start(f32[32,64,128]{2,1,0:T(8,128)} %multiply_add_fusion.2), channel_id=1, source_target_pairs={{0,4},{4,8},{8,12},{12,16},{16,20},{20,24},{24,28},{1,5},{5,9},{9,... | collective-permute-start | bytes 3145736 | tf_op jit(solution)/shard_map/while/body/eval_jaxpr/ppermute | solution.py:19
  650.5 16.4 %collective-permute-start = (f32[32,64,128]{2,1,0:T(8,128)}, f32[32,64,128]{2,1,0:T(8,128)}, u32[]{:S(2)}, u32[]{:S(2)}) collective-permute-start(f32[32,64,128]{2,1,0:T(8,128)} %multiply_add_fusion.2), channel_id=1, source_target_pairs={{0,4},{4,8},{8,12},{12,16},{16,20},{20,24},{24,28},{1,5},{5,9},{9,... | collective-permute-start | bytes 3145736 | tf_op jit(solution)/shard_map/while/body/eval_jaxpr/ppermute | solution.py:19
  669.3 16.4 %collective-permute-start = (f32[32,64,128]{2,1,0:T(8,128)}, f32[32,64,128]{2,1,0:T(8,128)}, u32[]{:S(2)}, u32[]{:S(2)}) collective-permute-start(f32[32,64,128]{2,1,0:T(8,128)} %multiply_add_fusion.2), channel_id=1, source_target_pairs={{0,4},{4,8},{8,12},{12,16},{16,20},{20,24},{24,28},{1,5},{5,9},{9,... | collective-permute-start | bytes 3145736 | tf_op jit(solution)/shard_map/while/body/eval_jaxpr/ppermute | solution.py:19
  757.5 121.0 %all-gather.20.cloned.1.call-start = ((), (), s32[]{:S(2)}) async-start(), calls=%async_computation.8 | async-start | bytes 5242880 | tf_op jit(solution)/shard_map/all_gather | solution.py:202
  890.5 7.7 collective-permute-start.5
  894.7 7.7 collective-permute-start.14
  921.2 7.8 collective-permute-start.9
  925.4 7.8 collective-permute-start.18
  929.0 15.0 %collective-permute-start.10 = (bf16[512,256]{1,0:T(8,128)(2,1)}, bf16[512,256]{1,0:T(8,128)(2,1)S(1)}, u32[]{:S(2)}, u32[]{:S(2)}) collective-permute-start(bf16[512,256]{1,0:T(8,128)(2,1)} %collective-permute-done.9), channel_id=1, source_target_pairs={{0,4},{4,8},{8,12},{12,16},{16,20},{20,24},{24,28},{1,5},{5,9},{9,... | collective-permute-start | bytes 786440 | tf_op jit(solution)/shard_map/ppermute | solution.py:19
  933.2 12.1 %collective-permute-start.19 = (bf16[512,256]{1,0:T(8,128)(2,1)}, bf16[512,256]{1,0:T(8,128)(2,1)S(1)}, u32[]{:S(2)}, u32[]{:S(2)}) collective-permute-start(bf16[512,256]{1,0:T(8,128)(2,1)} %collective-permute-done.18), channel_id=1, source_target_pairs={{0,4},{4,8},{8,12},{12,16},{16,20},{20,24},{24,28},{1,5},{5,9},{9,... | collective-permute-start | bytes 786440 | tf_op jit(solution)/shard_map/ppermute | solution.py:19
  944.0 8.3 collective-permute-start.11
  (61 other events, 1958.7 us)
Sparse Core Ops, SparseCore 0:
  9.9 53.3 all-gather.7
  64.9 28.1 all-gather.13
  94.7 28.5 all-gather.11
  124.8 148.9 all-gather.9
  275.2 149.6 all-gather.15
  426.3 154.5 all-gather.17
  757.6 64.7 reduce-scatter.1
  825.9 52.5 all-gather.19
where the time goes:
time: 1070 us; the launch traced here: 1050 us
  waiting for transfers between devices  489 us (46%)
  matrix products  224 us (21%)
  local copies, waits for them, and re-layouts  208 us (19%)
  other arithmetic  68.8 us (6%)
  starting transfers between devices  34.2 us (3%)
  between operations  15.2 us (1%)
  blocking collectives  14.7 us (1%)
    ppermute x26, waiting for transfers between devices, from_behind(): return lax.ppermute(block, axis, route)  151 us
    all_gather x1, waiting for transfers between devices, on_device(): lax.all_gather(w_x, 'seq', axis=0, tiled=True)  132 us
    dynamic_update_slice x4, local copies, waits for them, and re-layouts, run_ssd(): lax.scan(ssd_block, carry_state, (blocked(inputs), blocked(step_sizes), b...  106 us
    reduce_scatter x1, waiting for transfers between devices, on_device(): lax.psum_scatter(rounded.astype(jnp.bfloat16), 'mp', scatter_dimension=1,...  64.8 us
    all_gather x1, waiting for transfers between devices, on_device(): stream_rows = lax.all_gather(mixed_low, 'mp', axis=1, tiled=True)  52.7 us
    dot_general x5, matrix products, add_rows(): return jnp.dot(normed, piece, preferred_element_type=jnp.float32)  41.2 us
    dot_general x8, matrix products, one_head(): lax.dot_general(query_h, key_h, (((1,), (1,)), ((), ())), preferred_eleme...  40.1 us
    all_gather x1, waiting for transfers between devices, on_device(): whole_rows = lax.all_gather(hidden_in, 'mp', axis=1, tiled=True)  34.9 us
  transfers between devices with their start and end apart: 34, of which 26 were waited for; matrix products, arithmetic and copies ran while one was open for 36% of the time, Pallas kernels for 0%

commit v1 on v0

v1 whole, which is shorter than its diff:
```python
import functools
import math

import jax
import jax.numpy as jnp
from jax import lax
from jax.experimental import pallas as pl
from jax.experimental.pallas import tpu as pltpu
from jax.sharding import PartitionSpec as P

P_SIZE = 64
N = 128
HD = 128
WINDOW = 4096
QB = 128
LANES = 128
VMEM_LIMIT = 62 * 1024 * 1024

HIGH = lax.Precision.HIGHEST
F32 = jnp.float32
BF16 = jnp.bfloat16


def from_behind(block, axis, distance):
    devices = range(lax.axis_size(axis))
    route = [(i - distance, i) for i in devices if i - distance in devices]
    return lax.ppermute(block, axis, route)


def rms_norm(values, gain):
    return values * lax.rsqrt(jnp.mean(values * values, axis=-1, keepdims=True) + 1e-05) * gain


def signal_seq(sem, index):
    pl.semaphore_signal(
        sem, inc=1, device_id={"seq": index}, device_id_type=pl.DeviceIdType.MESH
    )


def gather_dot_kernel(n, normed_ref, w_ref, out_ref, slots, local_sem, send_sem, recv_sem):
    me = lax.axis_index("seq")
    ring = n // 2
    half = ring // 2
    chip, core = me // 2, lax.rem(me, 2)
    up = lax.rem(chip + 1, ring) * 2 + core
    down = lax.rem(chip + ring - 1, ring) * 2 + core
    partner = chip * 2 + 1 - core
    depth, cols = w_ref.shape
    mid = depth // 2

    barrier = pltpu.get_barrier_semaphore()
    for other in (up, down, partner):
        signal_seq(barrier, other)
    pl.semaphore_wait(barrier, 3)

    local = pltpu.make_async_copy(w_ref, slots.at[0], local_sem)
    local.start()
    started = []

    def send(source, slot, rows, part, target):
        copy = pltpu.make_async_remote_copy(
            src_ref=source,
            dst_ref=slots.at[slot, rows],
            send_sem=send_sem.at[len(started)],
            recv_sem=recv_sem.at[2 * slot + part],
            device_id={"seq": target},
            device_id_type=pl.DeviceIdType.MESH,
        )
        copy.start()
        started.append(copy)

    def arrived(slot, rows, part):
        pltpu.make_async_copy(
            slots.at[slot, rows], slots.at[slot, rows], recv_sem.at[2 * slot + part]
        ).wait()

    whole, upper, lower = pl.ds(0, depth), pl.ds(0, mid), pl.ds(mid, mid)
    send(w_ref, 2 * 1, whole, 0, up)
    send(w_ref, 2 * (ring - 1), whole, 0, down)
    send(w_ref, 1, whole, 0, partner)

    def multiply(slot, first=False):
        step, lane = slot // 2, slot % 2
        origin = lax.rem(chip - step + ring, ring) * 2
        owner = origin + (core if lane == 0 else 1 - core)
        features = pl.ds(pl.multiple_of(owner * depth, depth), depth)

        def tile(start, width):
            where = pl.ds(start, width)
            product = jnp.dot(
                normed_ref[:, features], slots[slot, :, where], preferred_element_type=F32
            )
            if first:
                out_ref[:, where] = product
            else:
                out_ref[:, where] += product

        width = 512
        full = cols // width

        def body(i, carry):
            tile(pl.multiple_of(i * width, width), width)
            return carry

        lax.fori_loop(0, full, body, 0)
        if cols % width:
            tile(full * width, cols % width)

    local.wait()
    multiply(0, True)
    arrived(1, whole, 0)
    multiply(1)
    for d in range(1, half):
        s_up, s_down = 2 * d, 2 * (ring - d)
        last = d + 1 == half
        arrived(s_up, whole, 0)
        rows = upper if last else whole
        send(slots.at[s_up, rows], 2 * (d + 1), rows, 0, up)
        arrived(s_down, whole, 0)
        rows = lower if last else whole
        send(slots.at[s_down, rows], 2 * (ring - d - 1), rows, 1 if last else 0, down)
        send(slots.at[s_up, whole], s_up + 1, whole, 0, partner)
        send(slots.at[s_down, whole], s_down + 1, whole, 0, partner)
        multiply(s_up)
        multiply(s_down)
        arrived(s_up + 1, whole, 0)
        multiply(s_up + 1)
        arrived(s_down + 1, whole, 0)
        multiply(s_down + 1)
    far = 2 * half
    arrived(far, upper, 0)
    send(slots.at[far, upper], far + 1, upper, 0, partner)
    arrived(far, lower, 1)
    send(slots.at[far, lower], far + 1, lower, 1, partner)
    multiply(far)
    arrived(far + 1, upper, 0)
    arrived(far + 1, lower, 1)
    multiply(far + 1)
    for copy in started:
        copy.wait_send()


def gather_dot(normed, weights):
    n = lax.axis_size("seq")
    depth, cols = weights.shape
    ring = n // 2
    sends = 3 + 4 * (ring // 2 - 1) + 2
    return pl.pallas_call(
        functools.partial(gather_dot_kernel, n),
        out_shape=jax.ShapeDtypeStruct((normed.shape[0], cols), F32),
        in_specs=[
            pl.BlockSpec(memory_space=pltpu.VMEM),
            pl.BlockSpec(memory_space=pl.ANY),
        ],
        out_specs=pl.BlockSpec(memory_space=pltpu.VMEM),
        scratch_shapes=[
            pltpu.VMEM((n, depth, cols), BF16),
            pltpu.SemaphoreType.DMA,
            pltpu.SemaphoreType.DMA((sends,)),
            pltpu.SemaphoreType.DMA((2 * n,)),
        ],
        compiler_params=pltpu.CompilerParams(
            collective_id=0, has_side_effects=True, vmem_limit_bytes=VMEM_LIMIT
        ),
        cost_estimate=pl.CostEstimate(
            flops=2 * normed.shape[0] * normed.shape[1] * cols,
            bytes_accessed=160_000_000,
            transcendentals=0,
        ),
    )(normed, weights)


def silu(v):
    return v / (1.0 + jnp.exp(-v))


def spread_heads(values, expand):
    high = values.astype(BF16)
    low = (values - high.astype(F32)).astype(BF16)
    return jnp.dot(high, expand, preferred_element_type=F32) + jnp.dot(
        low, expand, preferred_element_type=F32
    )


def mixer_kernel(
    n,
    heads,
    groups,
    proj_ref,
    rim_ref,
    taps_ref,
    bias_ref,
    rate_ref,
    skip_ref,
    gain_ref,
    expand_ref,
    y_ref,
    window,
    conv,
    ssd,
    reads,
    logs,
    state,
    carry,
    state_out,
    carry_out,
    state_in,
    carry_in,
    send_sem,
    recv_sem,
):
    me = lax.axis_index("seq")
    rows = proj_ref.shape[0]
    inner = heads * P_SIZE
    width = inner + 2 * groups * N
    gate_at = width + LANES
    per_group = inner // groups
    blocks = rows // QB
    kw = taps_ref.shape[0]

    barrier = pltpu.get_barrier_semaphore()
    for d in range(1, n):
        signal_seq(barrier, lax.rem(me + d, n))
    pl.semaphore_wait(barrier, n - 1)

    expand = expand_ref[...]
    window[0:8, :] = rim_ref[...]
    state[...] = jnp.zeros_like(state)
    carry[...] = jnp.zeros_like(carry)
    row_id = lax.broadcasted_iota(jnp.int32, (QB, QB), 0)
    col_id = lax.broadcasted_iota(jnp.int32, (QB, QB), 1)
    causal = row_id >= col_id
    low_lanes = col_id < P_SIZE
    tri = jnp.where(causal, 1.0, 0.0).astype(F32)

    def block(i, carry_none):
        base = pl.multiple_of(i * QB, QB)
        here = pl.ds(base, QB)
        window[8 : 8 + QB, :] = proj_ref[here, 0:width]
        step_cols = 256 if width % 256 == 0 else 128
        for at in range(0, width, step_cols):
            cs = slice(at, at + step_cols)
            total = None
            for j in range(kw):
                term = taps_ref[j : j + 1, cs] * window[8 - kw + 1 + j : 8 - kw + 1 + j + QB, cs]
                total = term if total is None else total + term
            conv[:, cs] = silu(total)
        window[0:8, :] = window[QB : QB + 8, :]

        raw = proj_ref[here, width : width + LANES] + bias_ref[...]
        steps = jnp.maximum(raw, 0.0) + jnp.log1p(jnp.exp(-jnp.abs(raw)))
        decays = -rate_ref[...] * steps
        cum = jnp.dot(tri, decays, precision=HIGH, preferred_element_type=F32)
        cum_t = jnp.transpose(cum)
        logs[here, :] = cum + carry[0:1, :]
        carry[...] = carry[...] + cum[QB - 1 : QB, :]
        grown = jnp.exp(cum)
        tail = jnp.exp(cum[QB - 1 : QB, :] - cum)

        for g in range(groups):
            lanes = slice(g * per_group, (g + 1) * per_group)
            expand_g = expand[:, lanes]
            x = conv[:, lanes]
            b = conv[:, inner + g * N : inner + (g + 1) * N].astype(BF16)
            c = conv[:, inner + (groups + g) * N : inner + (groups + g + 1) * N].astype(BF16)
            reads[here, g * N : (g + 1) * N] = c
            scaled = x * spread_heads(steps, expand_g)
            grown_e = spread_heads(grown, expand_g)
            tailed = (scaled * spread_heads(tail, expand_g)).astype(BF16)
            scaled_low = scaled.astype(BF16)
            held = state[:, lanes]
            carried = grown_e * jnp.dot(c, held.astype(BF16), preferred_element_type=F32)
            ssd[here, lanes] = carried + skip_ref[:, lanes] * x
            fresh = lax.dot_general(
                b, tailed, (((0,), (0,)), ((), ())), preferred_element_type=F32
            )
            state[:, lanes] = grown_e[QB - 1 : QB, :] * held + fresh
            affinity = lax.dot_general(
                c, b, (((1,), (1,)), ((), ())), preferred_element_type=F32
            )
            affinity = jnp.where(causal, affinity, 0.0)
            for pair in range(per_group // LANES):
                at = pair * LANES
                inputs = scaled_low[:, at : at + LANES]
                outs = []
                for k in range(2):
                    h = (g * per_group + at) // P_SIZE + k
                    spread = jnp.minimum(cum[:, h : h + 1] - cum_t[h : h + 1, :], 0.0)
                    mixing = (affinity * jnp.exp(spread)).astype(BF16)
                    outs.append(jnp.dot(mixing, inputs, preferred_element_type=F32))
                where = slice(g * per_group + at, g * per_group + at + LANES)
                ssd[here, where] += jnp.where(low_lanes, outs[0], outs[1])
        return carry_none

    lax.fori_loop(0, blocks, block, 0)

    state_out[...] = state[...].astype(BF16)
    carry_out[...] = carry[...]

    def copies(d):
        target = lax.rem(me + d, n)
        return [
            pltpu.make_async_remote_copy(
                src_ref=source,
                dst_ref=slot.at[d - 1],
                send_sem=send_sem.at[2 * (d - 1) + k],
                recv_sem=recv_sem.at[2 * (d - 1) + k],
                device_id={"seq": target},
                device_id_type=pl.DeviceIdType.MESH,
            )
            for k, (source, slot) in enumerate(((state_out, state_in), (carry_out, carry_in)))
        ]

    for d in range(1, n):

        @pl.when(me + d < n)
        def _():
            for copy in copies(d):
                copy.start()

    state[...] = jnp.zeros_like(state)
    carry[...] = jnp.zeros_like(carry)
    for d in range(1, n):

        @pl.when(me - d >= 0)
        def _():
            for copy in copies(d):
                copy.wait_recv()
            weight = spread_heads(jnp.exp(carry[...]), expand)[0:1, :]
            state[...] += weight * state_in[d - 1].astype(F32)
            carry[...] += carry_in[d - 1]

    def finish(i, carry_none):
        here = pl.ds(pl.multiple_of(i * QB, QB), QB)
        grown = jnp.exp(logs[here, :])
        for g in range(groups):
            lanes = slice(g * per_group, (g + 1) * per_group)
            late = jnp.dot(
                reads[here, g * N : (g + 1) * N],
                state[:, lanes].astype(BF16),
                preferred_element_type=F32,
            )
            full = ssd[here, lanes] + spread_heads(grown, expand[:, lanes]) * late
            gate = proj_ref[here, gate_at + g * per_group : gate_at + (g + 1) * per_group]
            gated = full * silu(gate)
            power = jnp.mean(gated * gated, axis=-1, keepdims=True)
            y_ref[here, lanes] = (gated * lax.rsqrt(power + 1e-05) * gain_ref[:, lanes]).astype(BF16)
        return carry_none

    lax.fori_loop(0, blocks, finish, 0)
    for d in range(1, n):

        @pl.when(me + d < n)
        def _():
            for copy in copies(d):
                copy.wait_send()


def mixer(proj, rim, taps, bias, rate, skip, gain, heads, groups):
    n = lax.axis_size("seq")
    rows = proj.shape[0]
    inner = heads * P_SIZE
    width = inner + 2 * groups * N
    expand = (
        jnp.arange(LANES)[:, None] == (jnp.arange(inner) // P_SIZE)[None, :]
    ).astype(BF16)
    vmem = pl.BlockSpec(memory_space=pltpu.VMEM)
    return pl.pallas_call(
        functools.partial(mixer_kernel, n, heads, groups),
        out_shape=jax.ShapeDtypeStruct((rows, inner), BF16),
        in_specs=[vmem] * 8,
        out_specs=vmem,
        scratch_shapes=[
            pltpu.VMEM((8 + QB, width), F32),
            pltpu.VMEM((QB, width), F32),
            pltpu.VMEM((rows, inner), F32),
            pltpu.VMEM((rows, groups * N), BF16),
            pltpu.VMEM((rows, LANES), F32),
            pltpu.VMEM((N, inner), F32),
            pltpu.VMEM((8, LANES), F32),
            pltpu.VMEM((N, inner), BF16),
            pltpu.VMEM((8, LANES), F32),
            pltpu.VMEM((n - 1, N, inner), BF16),
            pltpu.VMEM((n - 1, 8, LANES), F32),
            pltpu.SemaphoreType.DMA((2 * (n - 1),)),
            pltpu.SemaphoreType.DMA((2 * (n - 1),)),
        ],
        compiler_params=pltpu.CompilerParams(
            collective_id=1, has_side_effects=True, vmem_limit_bytes=48 * 1024 * 1024
        ),
        cost_estimate=pl.CostEstimate(
            flops=8_000_000_000, bytes_accessed=100_000_000, transcendentals=8_000_000
        ),
    )(proj, rim, taps, bias, rate, skip, gain, expand)


def attention_kernel(n, rows, q_ref, k_ref, v_ref, o_ref, peak, total, acc):
    me = lax.axis_index("seq")
    reach = WINDOW // rows
    factor = HD ** (-0.5) * math.log2(math.e)
    query = q_ref[...]
    row_id = lax.broadcasted_iota(jnp.int32, (rows, rows), 0)
    col_id = lax.broadcasted_iota(jnp.int32, (rows, rows), 1)

    def visit(block, allowed, first):
        here = pl.ds(pl.multiple_of(block * rows, rows), rows)
        scores = lax.dot_general(
            query, k_ref[here, :], (((1,), (1,)), ((), ())), preferred_element_type=F32
        )
        if allowed is not None:
            scores = jnp.where(allowed, scores, -1e30)
        top = jnp.max(scores, axis=1, keepdims=True)
        if not first:
            before = peak[...]
            top = jnp.maximum(before, top)
        weights = jnp.exp2((scores - top) * factor)
        added = jnp.sum(weights, axis=1, keepdims=True)
        product = jnp.dot(weights.astype(BF16), v_ref[here, :], preferred_element_type=F32)
        if first:
            total[...] = added
            acc[...] = product
        else:
            shrink = jnp.exp2((before - top) * factor)
            total[...] = total[...] * shrink + added
            acc[...] = acc[...] * shrink + product
        peak[...] = top

    visit(me, row_id >= col_id, True)
    lowest = jnp.maximum(me - reach + 1, 0)

    def body(block, carry_none):
        visit(block, None, False)
        return carry_none

    lax.fori_loop(lowest, me, body, 0)
    if n > reach:

        @pl.when(me >= reach)
        def _():
            visit(me - reach, col_id > row_id, False)

    o_ref[...] = acc[...] / total[...]


def attention(queries, pairs, kv_heads):
    n = lax.axis_size("seq")
    rows = queries.shape[0]
    keys = pairs.shape[0]
    per_kv = queries.shape[1] // HD // kv_heads
    return pl.pallas_call(
        functools.partial(attention_kernel, n, rows),
        grid=(kv_heads, per_kv),
        out_shape=jax.ShapeDtypeStruct(queries.shape, F32),
        in_specs=[
            pl.BlockSpec((rows, HD), lambda i, j: (0, i * per_kv + j)),
            pl.BlockSpec((keys, HD), lambda i, j: (0, i)),
            pl.BlockSpec((keys, HD), lambda i, j: (0, kv_heads + i)),
        ],
        out_specs=pl.BlockSpec((rows, HD), lambda i, j: (0, i * per_kv + j)),
        scratch_shapes=[
            pltpu.VMEM((rows, 1), F32),
            pltpu.VMEM((rows, 1), F32),
            pltpu.VMEM((rows, HD), F32),
        ],
        compiler_params=pltpu.CompilerParams(
            dimension_semantics=("arbitrary", "arbitrary"), vmem_limit_bytes=40 * 1024 * 1024
        ),
        cost_estimate=pl.CostEstimate(
            flops=9_000_000_000, bytes_accessed=20_000_000, transcendentals=17_000_000
        ),
    )(queries, pairs, pairs)


def pad_lanes(values):
    return jnp.pad(values, ((0, 0), (0, LANES - values.shape[1])))


def on_device(
    hidden_in,
    norm_gain,
    w_z,
    w_x,
    w_b,
    w_c,
    w_dt,
    conv_x,
    conv_b,
    conv_c,
    dt_bias,
    a_rate,
    skip_gain,
    group_gain,
    w_out,
    attn_gain,
    w_q,
    w_k,
    w_v,
):
    whole_rows = lax.all_gather(hidden_in, "mp", axis=1, tiled=True)
    normed = rms_norm(whole_rows.astype(F32), norm_gain).astype(BF16)
    out_columns = lax.all_gather(w_out, "seq", axis=1, tiled=True)
    proj = gather_dot(
        normed, jnp.concatenate([w_x, w_b, w_c, pad_lanes(w_dt), w_z], axis=1)
    )
    heads = dt_bias.shape[0]
    groups = conv_b.shape[1] // N
    width = conv_x.shape[1] + conv_b.shape[1] + conv_c.shape[1]
    rim = from_behind(proj[proj.shape[0] - 8 :, :width], "seq", 1)
    y_normed = mixer(
        proj,
        rim,
        jnp.concatenate([conv_x, conv_b, conv_c], axis=1),
        pad_lanes(dt_bias[None, :]),
        pad_lanes(a_rate[None, :]),
        jnp.repeat(skip_gain, P_SIZE)[None, :],
        group_gain[None, :],
        heads,
        groups,
    )
    part = jnp.dot(y_normed, out_columns, preferred_element_type=F32).astype(BF16)
    summed = lax.psum_scatter(part, "mp", scatter_dimension=1, tiled=True).astype(F32)
    mixed = hidden_in.astype(F32) + summed
    mixed_low = mixed.astype(BF16)
    stream_rows = lax.all_gather(mixed_low, "mp", axis=1, tiled=True)
    normed_two = rms_norm(stream_rows.astype(F32), attn_gain).astype(BF16)
    own_keys = jnp.dot(normed_two, w_k, preferred_element_type=F32).astype(BF16)
    own_values = jnp.dot(normed_two, w_v, preferred_element_type=F32).astype(BF16)
    pairs = lax.all_gather(
        jnp.concatenate([own_keys, own_values], axis=1), "seq", axis=0, tiled=True
    )
    queries = jnp.dot(normed_two, w_q, preferred_element_type=F32).astype(BF16)
    context = attention(queries, pairs, own_keys.shape[1] // HD)
    return (mixed, context)


def solution(mesh):
    placed = (
        P("seq", "mp"),
        P(),
        P("seq", "mp"),
        P("seq", "mp"),
        P("seq", "mp"),
        P("seq", "mp"),
        P("seq", "mp"),
        P(None, "mp"),
        P(None, "mp"),
        P(None, "mp"),
        P("mp"),
        P("mp"),
        P("mp"),
        P("mp"),
        P("mp", "seq"),
        P(),
        P(None, "mp"),
        P(None, "mp"),
        P(None, "mp"),
    )
    return jax.shard_map(
        on_device,
        mesh=mesh,
        in_specs=placed,
        out_specs=(P("seq", "mp"), P("seq", "mp")),
        check_vma=False,
    )
```

time: 1070 us -> 925 us (0.86); the launches traced: 1050 us -> 924 us
  Pallas kernels: 0 us -> 661 us
  waiting for transfers between devices: 489 us -> 194 us
  local copies, waits for them, and re-layouts: 208 us -> 10.4 us
  matrix products: 224 us -> 28.6 us
  other arithmetic: 68.8 us -> 14.2 us
  starting transfers between devices: 34.2 us -> 1.48 us
  blocking collectives: 14.7 us -> 0 us
    pallas_call x0 -> x3, Pallas kernels: none -> 661 us  [the longest x1 465 us: gather_dot(): pl.pallas_call(functools.partial(gather_dot_kernel, n), out_shape=jax.Sha...]
    dot_general x42 -> x4, matrix products: 224 us -> 28.6 us  [the longest x1 14.4 us: on_device(): jnp.dot(y_normed, out_columns, preferred_element_type=F32).astype(BF16)]
    ppermute x26 -> x1, waiting for transfers between devices: 151 us -> 1.62 us  [from_behind(): return lax.ppermute(block, axis, route)]
    all_gather x5 -> x2, waiting for transfers between devices: 182 us -> 36.4 us  [the longest x1 36.4 us: on_device(): lax.all_gather(jnp.concatenate([own_keys, own_values], axis=1), 'seq', ax...]
    dynamic_update_slice x4 -> x0, local copies, waits for them, and re-layouts: 106 us -> none  [run_ssd(): lax.scan(ssd_block, carry_state, (blocked(inputs), blocked(step_sizes), b...]
    ppermute x26 -> x1, starting transfers between devices: 33.9 us -> 1.28 us  [from_behind(): return lax.ppermute(block, axis, route)]
    mul x7 -> x0, other arithmetic: 21.1 us -> none  [the longest x3 15 us: causal_conv(): return jax.nn.silu(summed)]
    broadcast_in_dim x12 -> x1, local copies, waits for them, and re-layouts: 20.1 us -> 0.07 us  [on_device(): jnp.repeat(skip_gain, P_SIZE)[None, :]]
  transfers between devices with their start and end apart: 34 -> 6, of which waited for: 26 -> 5; matrix products, arithmetic and copies ran while one was open for 36% -> 2% of each run, Pallas kernels for 0% -> 63%
where the time goes in v1:
time: 925 us; the launch traced here: 924 us
  Pallas kernels  661 us (71%)
  waiting for transfers between devices  194 us (21%)
  matrix products  28.6 us (3%)
  other arithmetic  14.2 us (2%)
  between operations  14.1 us (2%)
  local copies, waits for them, and re-layouts  10.4 us (1%)
    pallas_call x1, Pallas kernels, gather_dot(): pl.pallas_call(functools.partial(gather_dot_kernel, n), out_shape=jax.Sha...  465 us
    pallas_call x1, Pallas kernels, mixer(): pl.pallas_call(functools.partial(mixer_kernel, n, heads, groups), out_sha...  116 us
    pallas_call x1, Pallas kernels, attention(): pl.pallas_call(functools.partial(attention_kernel, n, rows), grid=(kv_hea...  79.5 us
    reduce_scatter x1, waiting for transfers between devices, on_device(): lax.psum_scatter(part, 'mp', scatter_dimension=1, tiled=True).astype(F32)  53 us
    all_gather x1, waiting for transfers between devices, on_device(): stream_rows = lax.all_gather(mixed_low, 'mp', axis=1, tiled=True)  52.7 us
    all_gather x1, waiting for transfers between devices, on_device(): whole_rows = lax.all_gather(hidden_in, 'mp', axis=1, tiled=True)  49.2 us
    all_gather x1, waiting for transfers between devices, on_device(): lax.all_gather(jnp.concatenate([own_keys, own_values], axis=1), 'seq', ax...  36.4 us
  transfers between devices with their start and end apart: 6, of which 5 were waited for; matrix products, arithmetic and copies ran while one was open for 2% of the time, Pallas kernels for 63%

profile of v1, /device:TPU:25, one launch (start us, length us, event | category | flops | bytes accessed | tf_op | source)
XLA Modules:
  0.0 924.1 jit_solution(17268101514936670979)
XLA Ops:
  8.7 0.9 copy.21
  9.6 1.8 constant_dynamic-update-slice_fusion.3
  11.7 2.3 copy-done.7
  14.1 49.2 %all-gather.5.cloned.1.call-done = bf16[512,4096]{1,0:T(8,128)(2,1)} async-done(((bf16[512,1024]{1,0:T(8,128)(2,1)}), bf16[512,4096]{1,0:T(8,128)(2,1)}) %all-gather.5.cloned.1.call-update) | async-done | bytes 4194320 | tf_op jit(solution)/shard_map/all_gather | solution.py:499
  63.3 3.2 fusion
  66.7 3.6 fusion.2.normed_ref
  70.3 465.4 %shard_map.194.proj_ref = f32[512,4736]{1,0:T(8,128)} custom-call(bf16[512,4096]{1,0:T(8,128)(2,1)} %fusion.2.normed_ref, bf16[512,4736]{1,0:T(8,128)(2,1)} %copy-done.7), custom_call_target="tpu_custom_call" | custom-call | flops 19864223744 | bytes 160000000 | tf_op jit(solution)/shard_map/pallas_call | solution.py:148
  535.7 0.9 slice.3
  536.6 1.3 collective-permute-start
  538.1 1.6 collective-permute-done.rim_ref
  539.8 116.1 %shard_map.195 = bf16[512,2048]{1,0:T(8,128)(2,1)S(1)} custom-call(f32[512,4736]{1,0:T(8,128)} %shard_map.194.proj_ref, f32[8,2560]{1,0:T(8,128)S(1)} %collective-permute-done.rim_ref, f32[4,2560]{1,0:T(4,128)S(1)} %pad_maximum_fusion.1.taps_ref, f32[1,128]{1,0:T(1,128)S(1)} %pad.12.bias_ref, f32[1,128]{1,0:T(1,128)S(1)} %pad.13.rate_ref, ...), custom_call_target="tpu_custom_call" | custom-call | flops 8000000000 | bytes 100000000 | tf_op jit(solution)/shard_map/pallas_call | solution.py:368
  655.9 1.3 copy-done.2
  657.2 14.4 %convolution_convert_fusion = bf16[512,4096]{1,0:T(8,128)(2,1)} fusion(bf16[512,2048]{1,0:T(8,128)(2,1)} %copy-done.2, bf16[2048,4096]{1,0:T(8,128)(2,1)} %all-gather.7.cloned.1.call-done), kind=kOutput, calls=%fused_computation.10 | convolution fusion | flops 8592031744 | bytes 23068672 | tf_op jit(solution)/shard_map/dot_general | solution.py:520
  671.7 53.0 %reduce-scatter.2.cloned.1.call-done = bf16[512,1024]{1,0:T(8,128)(2,1)} async-done(((bf16[512,4096]{1,0:T(8,128)(2,1)}), bf16[512,1024]{1,0:T(8,128)(2,1)}) %reduce-scatter.2.cloned.1.call-update) | async-done | bytes 1048592 | tf_op jit(solution)/shard_map/reduce_scatter | solution.py:521
  724.7 3.3 fusion.13
  728.1 52.7 %all-gather.9.cloned.1.call-done = bf16[512,4096]{1,0:T(8,128)(2,1)} async-done(((bf16[512,1024]{1,0:T(8,128)(2,1)}), bf16[512,4096]{1,0:T(8,128)(2,1)}) %all-gather.9.cloned.1.call-update) | async-done | bytes 4194320 | tf_op jit(solution)/shard_map/all_gather | solution.py:524
  780.8 3.1 fusion.3
  783.9 3.7 convolution_convert_fusion.3
  788.0 1.3 convolution_convert_fusion.2
  789.4 0.8 pad_maximum_fusion
  790.2 9.2 convolution_convert_fusion.1.q_ref
  799.4 36.4 %all-gather.11.cloned.1.call-done.k_ref.v_ref = bf16[4096,512]{1,0:T(8,128)(2,1)} async-done(((bf16[512,512]{1,0:T(8,128)(2,1)}), bf16[4096,512]{1,0:T(8,128)(2,1)}) %all-gather.11.cloned.1.call-update) | async-done | bytes 4194320 | tf_op jit(solution)/shard_map/all_gather | solution.py:528
  835.9 2.2 copy-done
  838.0 79.5 %shard_map.196 = f32[512,1024]{1,0:T(8,128)} custom-call(bf16[512,1024]{1,0:T(8,128)(2,1)S(1)} %convolution_convert_fusion.1.q_ref, bf16[4096,512]{1,0:T(8,128)(2,1)S(1)} %copy-done, bf16[4096,512]{1,0:T(8,128)(2,1)S(1)} %copy-done), custom_call_target="tpu_custom_call" | custom-call | flops 8999999488 | bytes 20000000 | tf_op jit(solution)/shard_map/pallas_call | solution.py:450
  (61 shorter events, 2.9 us)
Async XLA Ops:
  7.2 4.2 copy-start.8
  7.2 4.2 copy-start.9
  7.2 4.3 copy-start.6
  7.2 56.1 %all-gather.5.cloned.1.call-start = ((), (), s32[]{:S(2)}) async-start(), calls=%async_computation.1 | async-start | bytes 5242880 | tf_op jit(solution)/shard_map/all_gather | solution.py:499
  7.9 649.2 %all-gather.7.cloned.1.call-start = ((), (), s32[]{:S(2)}) async-start(), calls=%async_computation.2 | async-start | bytes 18874368 | tf_op jit(solution)/shard_map/all_gather | solution.py:501
  8.7 716.0 %reduce-scatter.2.cloned.1.call-start = ((), (), s32[]{:S(2)}) async-start(), calls=%async_computation.3 | async-start | bytes 5242880 | tf_op jit(solution)/shard_map/reduce_scatter | solution.py:521
  11.4 55.1 %copy-start.11 = (f32[4096]{0:T(1024)S(1)}, f32[4096]{0:T(1024)}, u32[]{:S(2)}) copy-start(f32[4096]{0:T(1024)} %param.20) | copy-start | bytes 49156
  11.7 2.3 copy-start.7
  63.3 3.4 copy-start.3
  70.3 467.6 %copy-start.10 = (f32[4,2048]{1,0:T(4,128)S(1)}, f32[4,2048]{1,0:T(4,128)}, u32[]{:S(2)}) copy-start(f32[4,2048]{1,0:T(4,128)} %param.26) | copy-start | bytes 98308
  70.3 467.6 %copy-start.12 = (f32[4,256]{1,0:T(4,128)S(1)}, f32[4,256]{1,0:T(4,128)}, u32[]{:S(2)}) copy-start(f32[4,256]{1,0:T(4,128)} %param.28) | copy-start | bytes 12292
  70.3 467.6 %copy-start.13 = (f32[4,256]{1,0:T(4,128)S(1)}, f32[4,256]{1,0:T(4,128)}, u32[]{:S(2)}) copy-start(f32[4,256]{1,0:T(4,128)} %param.27) | copy-start | bytes 12292
  70.3 467.6 %copy-start.14 = (f32[32]{0:T(128)S(1)}, f32[32]{0:T(128)}, u32[]{:S(2)}) copy-start(f32[32]{0:T(128)} %param.31) | copy-start | bytes 388
  70.3 467.8 %copy-start.18 = (f32[32]{0:T(128)S(1)}, f32[32]{0:T(128)}, u32[]{:S(2)}) copy-start(f32[32]{0:T(128)} %param.29) | copy-start | bytes 388
  70.3 467.8 %copy-start.19 = (f32[32]{0:T(128)S(1)}, f32[32]{0:T(128)}, u32[]{:S(2)}) copy-start(f32[32]{0:T(128)} %param.30) | copy-start | bytes 388
  70.3 469.4 %copy-start.1 = (f32[2048]{0:T(1024)S(1)}, f32[2048]{0:T(1024)}, u32[]{:S(2)}) copy-start(f32[2048]{0:T(1024)} %param.32) | copy-start | bytes 24580
  536.6 3.2 collective-permute-start
  671.6 53.1 %copy-start.4 = (bf16[512,1024]{1,0:T(8,128)(2,1)S(1)}, bf16[512,1024]{1,0:T(8,128)(2,1)}, u32[]{:S(2)}) copy-start(bf16[512,1024]{1,0:T(8,128)(2,1)} %param.19) | copy-start | bytes 3145732
  671.6 112.3 %copy-start.15 = (bf16[4096,256]{1,0:T(8,128)(2,1)S(1)}, bf16[4096,256]{1,0:T(8,128)(2,1)}, u32[]{:S(2)}) copy-start(bf16[4096,256]{1,0:T(8,128)(2,1)} %param.36) | copy-start | bytes 6291460
  671.6 112.3 %copy-start.17 = (f32[4096]{0:T(1024)S(1)}, f32[4096]{0:T(1024)}, u32[]{:S(2)}) copy-start(f32[4096]{0:T(1024)} %param.34) | copy-start | bytes 49156
  671.6 109.2 %all-gather.9.cloned.1.call-start = ((), (), s32[]{:S(2)}) async-start(), calls=%async_computation.4 | async-start | bytes 5242880 | tf_op jit(solution)/shard_map/all_gather | solution.py:524
  728.1 107.8 %all-gather.11.cloned.1.call-start = ((), (), s32[]{:S(2)}) async-start(), calls=%async_computation.5 | async-start | bytes 4718592 | tf_op jit(solution)/shard_map/all_gather | solution.py:528
  783.9 3.7 copy-start.5
  783.9 4.1 copy-start.16
  (2 other events, 3.5 us)
Sparse Core Ops, SparseCore 0:
  9.8 53.3 all-gather.4
  64.9 280.3 all-gather.6
  671.7 52.9 reduce-scatter.1
  728.2 52.5 all-gather.8
  790.3 45.4 all-gather.10

commit v2 on v1

--- a/solution.py
+++ b/solution.py
@@ -37,8 +37,70 @@
     )
 
 
-def gather_dot_kernel(n, normed_ref, w_ref, out_ref, slots, local_sem, send_sem, recv_sem):
+def signal_mp(sem, index):
+    pl.semaphore_signal(
+        sem, inc=1, device_id={"mp": index}, device_id_type=pl.DeviceIdType.MESH
+    )
+
+
+def norm_rows(source, gain_ref, target):
+    rows = source.shape[0]
+    tile = min(64, rows)
+
+    def body(i, carry_none):
+        here = pl.ds(pl.multiple_of(i * tile, tile), tile)
+        target[here, :] = rms_norm(source[here, :].astype(F32), gain_ref[...]).astype(BF16)
+        return carry_none
+
+    lax.fori_loop(0, rows // tile, body, 0)
+
+
+def share_features(m, source, whole, send_sem, recv_sem):
+    member = lax.axis_index("mp")
+    wide = source.shape[1]
+    own = pl.ds(pl.multiple_of(member * wide, wide), wide)
+    copies = [
+        pltpu.make_async_remote_copy(
+            src_ref=source,
+            dst_ref=whole.at[:, own],
+            send_sem=send_sem.at[d - 1],
+            recv_sem=recv_sem.at[d - 1],
+            device_id={"mp": lax.rem(member + d, m)},
+            device_id_type=pl.DeviceIdType.MESH,
+        )
+        for d in range(1, m)
+    ]
+    for copy in copies:
+        copy.start()
+    return copies, own
+
+
+def features_arrived(m, whole, wide, recv_sem):
+    member = lax.axis_index("mp")
+    for d in range(1, m):
+        sender = lax.rem(member - d + m, m)
+        there = whole.at[:, pl.ds(pl.multiple_of(sender * wide, wide), wide)]
+        pltpu.make_async_copy(there, there, recv_sem.at[d - 1]).wait()
+
+
+def gather_dot_kernel(
+    n,
+    m,
+    hidden_ref,
+    gain_ref,
+    w_ref,
+    out_ref,
+    slots,
+    normed_ref,
+    local_sem,
+    send_sem,
+    recv_sem,
+    own_sem,
+    mp_send_sem,
+    mp_recv_sem,
+):
     me = lax.axis_index("seq")
+    member = lax.axis_index("mp")
     ring = n // 2
     half = ring // 2
     chip, core = me // 2, lax.rem(me, 2)
@@ -51,8 +113,13 @@
     barrier = pltpu.get_barrier_semaphore()
     for other in (up, down, partner):
         signal_seq(barrier, other)
-    pl.semaphore_wait(barrier, 3)
-
+    for d in range(1, m):
+        signal_mp(barrier, lax.rem(member + d, m))
+    pl.semaphore_wait(barrier, 3 + m - 1)
+
+    shared, own = share_features(m, hidden_ref, normed_ref, mp_send_sem, mp_recv_sem)
+    own_copy = pltpu.make_async_copy(hidden_ref, normed_ref.at[:, own], own_sem)
+    own_copy.start()
     local = pltpu.make_async_copy(w_ref, slots.at[0], local_sem)
     local.start()
     started = []
@@ -106,6 +173,9 @@
         if cols % width:
             tile(full * width, cols % width)
 
+    own_copy.wait()
+    features_arrived(m, normed_ref, hidden_ref.shape[1], mp_recv_sem)
+    norm_rows(normed_ref, gain_ref, normed_ref)
     local.wait()
     multiply(0, True)
     arrived(1, whole, 0)
@@ -136,38 +206,44 @@
     arrived(far + 1, upper, 0)
     arrived(far + 1, lower, 1)
     multiply(far + 1)
-    for copy in started:
+    for copy in started + shared:
         copy.wait_send()
 
 
-def gather_dot(normed, weights):
-    n = lax.axis_size("seq")
+def gather_dot(hidden, gain, weights):
+    n, m = lax.axis_size("seq"), lax.axis_size("mp")
     depth, cols = weights.shape
+    rows, features = hidden.shape[0], hidden.shape[1] * m
     ring = n // 2
     sends = 3 + 4 * (ring // 2 - 1) + 2
     return pl.pallas_call(
-        functools.partial(gather_dot_kernel, n),
-        out_shape=jax.ShapeDtypeStruct((normed.shape[0], cols), F32),
+        functools.partial(gather_dot_kernel, n, m),
+        out_shape=jax.ShapeDtypeStruct((rows, cols), F32),
         in_specs=[
+            pl.BlockSpec(memory_space=pl.ANY),
             pl.BlockSpec(memory_space=pltpu.VMEM),
             pl.BlockSpec(memory_space=pl.ANY),
         ],
         out_specs=pl.BlockSpec(memory_space=pltpu.VMEM),
         scratch_shapes=[
             pltpu.VMEM((n, depth, cols), BF16),
+            pltpu.VMEM((rows, features), BF16),
             pltpu.SemaphoreType.DMA,
             pltpu.SemaphoreType.DMA((sends,)),
             pltpu.SemaphoreType.DMA((2 * n,)),
+            pltpu.SemaphoreType.DMA,
+            pltpu.SemaphoreType.DMA((m - 1,)),
+            pltpu.SemaphoreType.DMA((m - 1,)),
         ],
         compiler_params=pltpu.CompilerParams(
             collective_id=0, has_side_effects=True, vmem_limit_bytes=VMEM_LIMIT
         ),
         cost_estimate=pl.CostEstimate(
-            flops=2 * normed.shape[0] * normed.shape[1] * cols,
+            flops=2 * rows * features * cols,
             bytes_accessed=160_000_000,
             transcendentals=0,
         ),
-    )(normed, weights)
+    )(hidden, gain, weights)
 
 
 def silu(v):
@@ -394,6 +470,109 @@
     )(proj, rim, taps, bias, rate, skip, gain, expand)
 
 
+def output_kernel(
+    m,
+    y_ref,
+    w_ref,
+    hidden_ref,
+    gain_ref,
+    mixed_ref,
+    normed_ref,
+    outgoing,
+    incoming,
+    low,
+    part_send,
+    part_recv,
+    own_sem,
+    mp_send,
+    mp_recv,
+):
+    member = lax.axis_index("mp")
+    wide = hidden_ref.shape[1]
+    barrier = pltpu.get_barrier_semaphore()
+    for d in range(1, m):
+        signal_mp(barrier, lax.rem(member + d, m))
+    pl.semaphore_wait(barrier, m - 1)
+    tile = min(512, wide)
+
+    def part(target, store):
+        for at in range(0, wide, tile):
+            where = pl.ds(pl.multiple_of(target * wide + at, tile), tile)
+            term = jnp.dot(y_ref[...], w_ref[:, where], preferred_element_type=F32)
+            store(slice(at, at + tile), term.astype(BF16))
+
+    copies = []
+    for d in range(1, m):
+        target = lax.rem(member + d, m)
+
+        def keep(where, term):
+            outgoing[d - 1, :, where] = term
+
+        part(target, keep)
+        copy = pltpu.make_async_remote_copy(
+            src_ref=outgoing.at[d - 1],
+            dst_ref=incoming.at[d - 1],
+            send_sem=part_send.at[d - 1],
+            recv_sem=part_recv.at[d - 1],
+            device_id={"mp": target},
+            device_id_type=pl.DeviceIdType.MESH,
+        )
+        copy.start()
+        copies.append(copy)
+
+    def begin(where, term):
+        mixed_ref[:, where] = hidden_ref[:, where].astype(F32) + term.astype(F32)
+
+    part(member, begin)
+    for d in range(1, m):
+        copies[d - 1].wait_recv()
+        if d < m - 1:
+            mixed_ref[...] += incoming[d - 1].astype(F32)
+        else:
+            total = mixed_ref[...] + incoming[d - 1].astype(F32)
+            mixed_ref[...] = total
+            low[...] = total.astype(BF16)
+    shared, own = share_features(m, low, normed_ref, mp_send, mp_recv)
+    own_copy = pltpu.make_async_copy(low, normed_ref.at[:, own], own_sem)
+    own_copy.start()
+    own_copy.wait()
+    features_arrived(m, normed_ref, wide, mp_recv)
+    norm_rows(normed_ref, gain_ref, normed_ref)
+    for copy in copies + shared:
+        copy.wait_send()
+
+
+def output_stage(y, weights, hidden, gain):
+    m = lax.axis_size("mp")
+    rows, wide = hidden.shape
+    vmem = pl.BlockSpec(memory_space=pltpu.VMEM)
+    return pl.pallas_call(
+        functools.partial(output_kernel, m),
+        out_shape=(
+            jax.ShapeDtypeStruct((rows, wide), F32),
+            jax.ShapeDtypeStruct((rows, wide * m), BF16),
+        ),
+        in_specs=[vmem] * 4,
+        out_specs=(vmem, vmem),
+        scratch_shapes=[
+            pltpu.VMEM((m - 1, rows, wide), BF16),
+            pltpu.VMEM((m - 1, rows, wide), BF16),
+            pltpu.VMEM((rows, wide), BF16),
+            pltpu.SemaphoreType.DMA((m - 1,)),
+            pltpu.SemaphoreType.DMA((m - 1,)),
+            pltpu.SemaphoreType.DMA,
+            pltpu.SemaphoreType.DMA((m - 1,)),
+            pltpu.SemaphoreType.DMA((m - 1,)),
+        ],
+        compiler_params=pltpu.CompilerParams(
+            collective_id=2, has_side_effects=True, vmem_limit_bytes=56 * 1024 * 1024
+        ),
+        cost_estimate=pl.CostEstimate(
+            flops=2 * rows * y.shape[1] * wide * m, bytes_accessed=60_000_000, transcendentals=0
+        ),
+    )(y, weights, hidden, gain)
+
+
 def attention_kernel(n, rows, q_ref, k_ref, v_ref, o_ref, peak, total, acc):
     me = lax.axis_index("seq")
     reach = WINDOW // rows
@@ -496,12 +675,13 @@
     w_k,
     w_v,
 ):
-    whole_rows = lax.all_gather(hidden_in, "mp", axis=1, tiled=True)
-    normed = rms_norm(whole_rows.astype(F32), norm_gain).astype(BF16)
+    proj = gather_dot(
+        hidden_in,
+        norm_gain[None, :],
+        jnp.concatenate([w_x, w_b, w_c, pad_lanes(w_dt), w_z], axis=1),
+    )
+    proj, w_out = lax.optimization_barrier((proj, w_out))
     out_columns = lax.all_gather(w_out, "seq", axis=1, tiled=True)
-    proj = gather_dot(
-        normed, jnp.concatenate([w_x, w_b, w_c, pad_lanes(w_dt), w_z], axis=1)
-    )
     heads = dt_bias.shape[0]
     groups = conv_b.shape[1] // N
     width = conv_x.shape[1] + conv_b.shape[1] + conv_c.shape[1]
@@ -517,12 +697,7 @@
         heads,
         groups,
     )
-    part = jnp.dot(y_normed, out_columns, preferred_element_type=F32).astype(BF16)
-    summed = lax.psum_scatter(part, "mp", scatter_dimension=1, tiled=True).astype(F32)
-    mixed = hidden_in.astype(F32) + summed
-    mixed_low = mixed.astype(BF16)
-    stream_rows = lax.all_gather(mixed_low, "mp", axis=1, tiled=True)
-    normed_two = rms_norm(stream_rows.astype(F32), attn_gain).astype(BF16)
+    mixed, normed_two = output_stage(y_normed, out_columns, hidden_in, attn_gain[None, :])
     own_keys = jnp.dot(normed_two, w_k, preferred_element_type=F32).astype(BF16)
     own_values = jnp.dot(normed_two, w_v, preferred_element_type=F32).astype(BF16)
     pairs = lax.all_gather(

time: 925 us -> 837 us (0.905)
  waiting for transfers between devices: 194 us -> 50.4 us
  Pallas kernels: 661 us -> 742 us
  matrix products: 28.6 us -> 14 us
  other arithmetic: 14.2 us -> 0.96 us
    pallas_call x1, Pallas kernels: 116 us -> 222 us  [mixer(): pl.pallas_call(functools.partial(mixer_kernel, n, heads, groups), out_sha...]
    all_gather x2 -> x0, waiting for transfers between devices: 102 us -> none  [the longest x1 52.7 us: on_device(): stream_rows = lax.all_gather(mixed_low, 'mp', axis=1, tiled=True)]
    reduce_scatter x1 -> x0, waiting for transfers between devices: 53 us -> none  [on_device(): lax.psum_scatter(part, 'mp', scatter_dimension=1, tiled=True).astype(F32)]
    pallas_call x1 -> x2, Pallas kernels: 465 us -> 440 us  [the longest x1 330 us: gather_dot(): pl.pallas_call(functools.partial(gather_dot_kernel, n, m), out_shape=jax....]
    dot_general x1 -> x0, matrix products: 14.4 us -> none  [on_device(): jnp.dot(y_normed, out_columns, preferred_element_type=F32).astype(BF16)]
    all_gather x1, waiting for transfers between devices: 0.01 us -> 11.6 us  [on_device(): out_columns = lax.all_gather(w_out, 'seq', axis=1, tiled=True)]
  transfers between devices with their start and end apart: 6 -> 3, of which waited for: 5 -> 3; matrix products, arithmetic and copies ran while one was open for 2% -> 1% of each run, Pallas kernels for 63% -> 27%
where the time goes in v2:
time: 837 us
  Pallas kernels  742 us (89%)
  waiting for transfers between devices  50.4 us (6%)
  between operations  14.3 us (2%)
  matrix products  14 us (2%)
  local copies, waits for them, and re-layouts  13.6 us (2%)
    pallas_call x1, Pallas kernels, gather_dot(): pl.pallas_call(functools.partial(gather_dot_kernel, n, m), out_shape=jax....  330 us
    pallas_call x1, Pallas kernels, mixer(): pl.pallas_call(functools.partial(mixer_kernel, n, heads, groups), out_sha...  222 us
    pallas_call x1, Pallas kernels, output_stage(): pl.pallas_call(functools.partial(output_kernel, m), out_shape=(jax.ShapeD...  110 us
    pallas_call x1, Pallas kernels, attention(): pl.pallas_call(functools.partial(attention_kernel, n, rows), grid=(kv_hea...  79.5 us
    all_gather x1, waiting for transfers between devices, on_device(): lax.all_gather(jnp.concatenate([own_keys, own_values], axis=1), 'seq', ax...  37.3 us
  transfers between devices with their start and end apart: 3, of which 3 were waited for; matrix products, arithmetic and copies ran while one was open for 1% of the time, Pallas kernels for 27%

profile of v2, /device:TPU:25, one launch (start us, length us, event | category | flops | bytes accessed | tf_op | source)
XLA Modules:
  0.0 836.8 jit_solution(4566226883233153769)
XLA Ops:
  7.3 3.4 constant_dynamic-update-slice_fusion.3
  10.6 0.1 copy.21
  10.8 0.8 constant_dynamic-update-slice_fusion.2
  11.5 0.7 constant_dynamic-update-slice_fusion.1
  12.3 0.7 pad_dynamic-update-slice_fusion
  13.0 1.5 constant_dynamic-update-slice_fusion.w_ref
  14.5 330.2 %shard_map.194.proj_ref = f32[512,4736]{1,0:T(8,128)} custom-call(bf16[512,1024]{1,0:T(8,128)(2,1)} %hidden_ref.3, f32[1,4096]{1,0:T(1,128)} %bitcast.12, bf16[512,4736]{1,0:T(8,128)(2,1)} %constant_dynamic-update-slice_fusion.w_ref), custom_call_target="tpu_custom_call" | custom-call | flops 19864223744 | bytes 160000000 | tf_op jit(solution)/shard_map/pallas_call | solution.py:219
  344.8 0.9 slice.3
  345.7 1.3 collective-permute-start
  347.0 0.1 fusion.expand_ref
  347.3 1.5 collective-permute-done.rim_ref
  348.8 222.2 %shard_map.195.y_ref = bf16[512,2048]{1,0:T(8,128)(2,1)S(1)} custom-call(f32[512,4736]{1,0:T(8,128)} %shard_map.194.proj_ref, f32[8,2560]{1,0:T(8,128)S(1)} %collective-permute-done.rim_ref, f32[4,2560]{1,0:T(4,128)S(1)} %pad_maximum_fusion.1.taps_ref, f32[1,128]{1,0:T(1,128)S(1)} %pad.12.bias_ref, f32[1,128]{1,0:T(1,128)S(1)} %pad.13.rate_ref, ...), custom_call_target="tpu_custom_call" | custom-call | flops 8000000000 | bytes 100000000 | tf_op jit(solution)/shard_map/pallas_call | solution.py:444
  571.1 1.3 copy-done.2
  572.4 11.6 %all-gather.3.cloned.1.call-done.w_ref = bf16[2048,4096]{1,0:T(8,128)(2,1)} async-done(((bf16[2048,512]{1,0:T(8,128)(2,1)}), bf16[2048,4096]{1,0:T(8,128)(2,1)}) %all-gather.3.cloned.1.call-update) | async-done | bytes 16777232 | tf_op jit(solution)/shard_map/all_gather | solution.py:684
  584.0 110.3 %shard_map.196 = (f32[512,1024]{1,0:T(8,128)}, bf16[512,4096]{1,0:T(8,128)(2,1)}) custom-call(bf16[512,2048]{1,0:T(8,128)(2,1)} %copy-done.2, bf16[2048,4096]{1,0:T(8,128)(2,1)} %all-gather.3.cloned.1.call-done.w_ref, bf16[512,1024]{1,0:T(8,128)(2,1)} %hidden_ref.3, f32[1,4096]{1,0:T(1,128)} %bitcast.13), custom_call_target="tpu_custom_call" | custom-call | flops 8589934592 | bytes 60000000 | tf_op jit(solution)/shard_map/pallas_call | solution.py:549
  694.4 3.6 convolution_convert_fusion.1
  698.0 0.5 copy-done.16
  698.4 1.2 convolution_convert_fusion.2
  699.7 0.8 pad_maximum_fusion
  700.5 9.1 %convolution_convert_fusion.q_ref = bf16[512,1024]{1,0:T(8,128)(2,1)S(1)} fusion(bf16[512,4096]{1,0:T(8,128)(2,1)} %get-tuple-element.9, bf16[4096,1024]{1,0:T(8,128)(2,1)} %param.35), kind=kOutput, calls=%fused_computation | convolution fusion | flops 4295491584 | bytes 13631488 | tf_op jit(solution)/shard_map/dot_general | solution.py:706
  709.7 37.3 %all-gather.5.cloned.1.call-done.k_ref.v_ref = bf16[4096,512]{1,0:T(8,128)(2,1)} async-done(((bf16[512,512]{1,0:T(8,128)(2,1)}), bf16[4096,512]{1,0:T(8,128)(2,1)}) %all-gather.5.cloned.1.call-update) | async-done | bytes 4194320 | tf_op jit(solution)/shard_map/all_gather | solution.py:703
  746.9 2.2 copy-done
  749.1 79.5 %shard_map.197 = f32[512,1024]{1,0:T(8,128)} custom-call(bf16[512,1024]{1,0:T(8,128)(2,1)S(1)} %convolution_convert_fusion.q_ref, bf16[4096,512]{1,0:T(8,128)(2,1)S(1)} %copy-done, bf16[4096,512]{1,0:T(8,128)(2,1)S(1)} %copy-done), custom_call_target="tpu_custom_call" | custom-call | flops 8999999488 | bytes 20000000 | tf_op jit(solution)/shard_map/pallas_call | solution.py:629
  828.7 1.3 copy.31
  (41 shorter events, 0.4 us)
Async XLA Ops:
  7.2 3.5 copy-start.7
  7.2 3.6 copy-start.5
  7.2 4.4 copy-start.6
  7.2 5.8 copy-start.3
  7.2 576.8 %all-gather.3.cloned.1.call-start = ((), (), s32[]{:S(2)}) async-start(), calls=%async_computation | async-start | bytes 18874368 | tf_op jit(solution)/shard_map/all_gather | solution.py:684
  14.5 332.6 %copy-start.8 = (f32[4,2048]{1,0:T(4,128)S(1)}, f32[4,2048]{1,0:T(4,128)}, u32[]{:S(2)}) copy-start(f32[4,2048]{1,0:T(4,128)} %param.26) | copy-start | bytes 98308
  14.5 332.6 %copy-start.9 = (f32[4,256]{1,0:T(4,128)S(1)}, f32[4,256]{1,0:T(4,128)}, u32[]{:S(2)}) copy-start(f32[4,256]{1,0:T(4,128)} %param.28) | copy-start | bytes 12292
  14.5 332.6 %copy-start.10 = (f32[4,256]{1,0:T(4,128)S(1)}, f32[4,256]{1,0:T(4,128)}, u32[]{:S(2)}) copy-start(f32[4,256]{1,0:T(4,128)} %param.27) | copy-start | bytes 12292
  14.5 332.6 %copy-start.11 = (f32[32]{0:T(128)S(1)}, f32[32]{0:T(128)}, u32[]{:S(2)}) copy-start(f32[32]{0:T(128)} %param.31) | copy-start | bytes 388
  14.5 332.8 %copy-start.14 = (f32[32]{0:T(128)S(1)}, f32[32]{0:T(128)}, u32[]{:S(2)}) copy-start(f32[32]{0:T(128)} %param.29) | copy-start | bytes 388
  14.5 332.8 %copy-start.15 = (f32[32]{0:T(128)S(1)}, f32[32]{0:T(128)}, u32[]{:S(2)}) copy-start(f32[32]{0:T(128)} %param.30) | copy-start | bytes 388
  14.5 334.3 %copy-start.1 = (f32[2048]{0:T(1024)S(1)}, f32[2048]{0:T(1024)}, u32[]{:S(2)}) copy-start(f32[2048]{0:T(1024)} %param.32) | copy-start | bytes 24580
  344.7 402.2 %all-gather.5.cloned.1.call-start = ((), (), s32[]{:S(2)}) async-start(), calls=%async_computation.1 | async-start | bytes 4718592 | tf_op jit(solution)/shard_map/all_gather | solution.py:703
  345.7 3.2 collective-permute-start
  571.1 1.3 copy-start.2
  584.0 110.3 %copy-start.12 = (bf16[4096,256]{1,0:T(8,128)(2,1)S(1)}, bf16[4096,256]{1,0:T(8,128)(2,1)}, u32[]{:S(2)}) copy-start(bf16[4096,256]{1,0:T(8,128)(2,1)} %param.37) | copy-start | bytes 6291460
  694.3 3.6 copy-start.13
  694.4 4.1 copy-start.16
  746.9 2.2 copy-start
  749.1 79.6 %copy-start.4 = (f32[512,1024]{1,0:T(8,128)S(1)}, f32[512,1024]{1,0:T(8,128)}, u32[]{:S(2)}) copy-start(f32[512,1024]{1,0:T(8,128)} %get-tuple-element.12) | copy-start | bytes 6291460
Sparse Core Ops, SparseCore 0:
  344.9 239.1 all-gather.2
  700.7 46.2 all-gather.4
